TPU v7x, 256 devices: a whole 4x4x8 slice. The times are simulated.
256 devices in a mesh: gx: 8 (over y, x_hi), gy: 32 (over z, x_lo, core).
Axes of the slice: x: 4 (x_hi: 2, x_lo: 2; x = x_hi * 2 + x_lo), y: 4, z: 8, core: 2. Of those that a mesh axis runs over, the one named last changes fastest.
Arguments:
- species_means: bfloat16 [8, 64, 120, 1024], P(None, 'gy', None, 'gx'), may hold values from 0.19921875 to 5
- zonal_edge_velocity: float32 [64, 120, 1024], P('gy', None, 'gx'), may hold values from -6 to 6
- meridional_edge_velocity: float32 [64, 120, 1024], P('gy', None, 'gx'), may hold values from -6 to 6
- scaled_warmth: float32 [64, 120, 1024], P('gy', None, 'gx'), may hold values from 0.5 to 2
- donor_depths: float32 [64, 120, 1024], P('gy', None, 'gx'), may hold values from 0.5 to 2
- leading_donor_level: int32 [64, 120, 1024], P('gy', None, 'gx'), may hold values from 0 to 118, as said below
- opening_share: bfloat16 [64, 120, 1024], P('gy', None, 'gx'), may hold values from 0 to 0.44921875
- closing_share: bfloat16 [64, 120, 1024], P('gy', None, 'gx'), may hold values from 0.546875 to 1
Outputs:
- tracers_out: float32 [8, 64, 120, 1024], P(None, 'gy', None, 'gx')
- regridded_zonal: float32 [64, 120, 1024], P('gy', None, 'gx')
- regridded_meridional: float32 [64, 120, 1024], P('gy', None, 'gx')
- adjusted_warmth: float32 [64, 120, 1024], P('gy', None, 'gx')
Inputs may be any that keep to these rules, and one draw needn't show every extreme that they name: Target layer k draws on source layers leading_donor_level and leading_donor_level + 1, and leading_donor_level lies within 2 of k.
All inputs are finite; a program needn't handle non-finite values.
Results may differ from a plain program's by a relative error of at most 0.0003.
Values sent between devices are 32-bit elements; how exact they have to be, the bound alone decides.
No kernel may reach another device: no remote copies, remote signals or barrier semaphores. Data moves between devices by JAX's collectives and lax.ppermute only.
A program may use at most 64 MiB of HBM per device.

v0:
```python
import jax
import jax.numpy as jnp
from jax import lax
from jax.sharding import Mesh
from jax.sharding import PartitionSpec as P

GY = ("gy_0", "gy_1", "gy_2")
GX = ("gx_0", "gx_1")
GX_GY = ("gx_0", "gx_1", "gy_0", "gy_1", "gy_2")
thermal_rescale_factor = 3.5
offsets_all = (-2, -1, 0, 1, 2, 3)


def passed_along(value, axis, steps):
    count = lax.axis_size(axis)
    pairs = [(source, (source + steps) % count) for source in range(count)]
    return lax.ppermute(value, axis, pairs)


def over_axes(x, axes):
    for axis in axes:
        x = lax.psum(x, axis)
    return x


def ppm_parts(values):
    layers = values.shape[-2]
    top_edge = 1.5 * values[..., 0:1, :] - 0.5 * values[..., 1:2, :]
    second_edge = 0.5 * (values[..., 0:1, :] + values[..., 1:2, :])
    inner_edge = 7.0 / 12.0 * (
        values[..., 1 : layers - 2, :] + values[..., 2 : layers - 1, :]
    ) - 1.0 / 12.0 * (values[..., 0 : layers - 3, :] + values[..., 3:layers, :])
    lower_edge = 0.5 * (
        values[..., layers - 2 : layers - 1, :] + values[..., layers - 1 : layers, :]
    )
    bottom_edge = (
        1.5 * values[..., layers - 1 : layers, :] - 0.5 * values[..., layers - 2 : layers - 1, :]
    )
    edge_values = jnp.concatenate(
        [top_edge, second_edge, inner_edge, lower_edge, bottom_edge], axis=-2
    )
    left_edge = edge_values[..., :layers, :]
    right_edge = edge_values[..., 1:, :]
    return (left_edge, right_edge - left_edge, 6.0 * values - 3.0 * (left_edge + right_edge))


def shifted_layers(values, amount):
    layers = values.shape[-2]
    if amount == 0:
        return values
    if amount > 0:
        filler = jnp.zeros(values.shape[:-2] + (amount, values.shape[-1]), values.dtype)
        return jnp.concatenate([values[..., amount:, :], filler], axis=-2)
    filler = jnp.zeros(values.shape[:-2] + (-amount, values.shape[-1]), values.dtype)
    return jnp.concatenate([filler, values[..., : layers + amount, :]], axis=-2)


def pick_layers(values, masks):
    total = jnp.zeros(values.shape, jnp.float32)
    for amount, selector in zip(offsets_all, masks):
        total = total + jnp.where(selector, shifted_layers(values, amount), 0.0)
    return total


def build_operator(donor_depths, leading_donor_level, opening_share, closing_share):
    start_frac = opening_share.astype(jnp.float32)
    end_frac = closing_share.astype(jnp.float32)
    layer_offset = leading_donor_level - lax.broadcasted_iota(
        jnp.int32, leading_donor_level.shape, 1
    )
    first_masks = [layer_offset == amount for amount in offsets_all]
    second_masks = [layer_offset + 1 == amount for amount in offsets_all]
    weight_first = (1.0 - start_frac) * pick_layers(donor_depths, first_masks)
    weight_second = end_frac * pick_layers(donor_depths, second_masks)
    linear_first = 0.5 * (start_frac + 1.0)
    square_first = linear_first - (start_frac * start_frac + start_frac + 1.0) / 3.0
    linear_second = 0.5 * end_frac
    square_second = linear_second - end_frac * end_frac / 3.0
    return (
        first_masks,
        second_masks,
        weight_first,
        weight_second,
        linear_first,
        square_first,
        linear_second,
        square_second,
    )


def multiply_by_regrid_operator(operator, values):
    (
        first_masks,
        second_masks,
        weight_first,
        weight_second,
        linear_first,
        square_first,
        linear_second,
        square_second,
    ) = operator
    left_edge, edge_slope, curvature = ppm_parts(values)
    mean_first = (
        pick_layers(left_edge, first_masks)
        + pick_layers(edge_slope, first_masks) * linear_first
        + pick_layers(curvature, first_masks) * square_first
    )
    mean_second = (
        pick_layers(left_edge, second_masks)
        + pick_layers(edge_slope, second_masks) * linear_second
        + pick_layers(curvature, second_masks) * square_second
    )
    return (weight_first * mean_first + weight_second * mean_second) / (
        weight_first + weight_second
    )


def local(
    species_means,
    zonal_edge_velocity,
    meridional_edge_velocity,
    scaled_warmth,
    donor_depths,
    leading_donor_level,
    opening_share,
    closing_share,
):
    vertical_regrid_operator = build_operator(
        donor_depths, leading_donor_level, opening_share, closing_share
    )
    regridded_depths = vertical_regrid_operator[2] + vertical_regrid_operator[3]
    mass_before = jnp.sum(species_means.astype(jnp.float32) * donor_depths, axis=(1, 2, 3))
    interior_u_faces = 0.5 * jnp.sum(
        0.5
        * (donor_depths[:-1] + donor_depths[1:])
        * zonal_edge_velocity[:-1]
        * zonal_edge_velocity[:-1]
    )
    interior_v_faces = 0.5 * jnp.sum(
        0.5
        * (donor_depths[:, :, :-1] + donor_depths[:, :, 1:])
        * meridional_edge_velocity[:, :, :-1]
        * meridional_edge_velocity[:, :, :-1]
    )
    local_prior_totals = (
        thermal_rescale_factor * jnp.sum(donor_depths * scaled_warmth)
        + interior_u_faces
        + interior_v_faces
    )
    from_south = passed_along(zonal_edge_velocity[-1:], GY, 1)
    u_paired = multiply_by_regrid_operator(
        vertical_regrid_operator,
        jnp.stack(
            [zonal_edge_velocity, jnp.concatenate([from_south, zonal_edge_velocity[:-1]], axis=0)]
        ),
    )
    u_cross = u_paired[1]
    returned = passed_along(
        jnp.stack([u_cross[0:1], donor_depths[0:1], regridded_depths[0:1]]), GY, -1
    )
    north_thick = returned[2]
    edge_u = 0.5 * jnp.sum(
        0.5
        * (donor_depths[-1:] + returned[1])
        * zonal_edge_velocity[-1:]
        * zonal_edge_velocity[-1:]
    )
    regridded_zonal = 0.5 * (u_paired[0] + jnp.concatenate([u_cross[1:], returned[0]], axis=0))
    zonal_following = 0.5 * jnp.sum(
        0.5
        * (regridded_depths + jnp.concatenate([regridded_depths[1:], north_thick], axis=0))
        * regridded_zonal
        * regridded_zonal
    )
    from_west = passed_along(meridional_edge_velocity[:, :, -1:], GX, 1)
    v_paired = multiply_by_regrid_operator(
        vertical_regrid_operator,
        jnp.stack(
            [
                meridional_edge_velocity,
                jnp.concatenate([from_west, meridional_edge_velocity[:, :, :-1]], axis=2),
            ]
        ),
    )
    v_cross = v_paired[1]
    v_returned = passed_along(
        jnp.stack([v_cross[:, :, 0:1], donor_depths[:, :, 0:1], regridded_depths[:, :, 0:1]]),
        GX,
        -1,
    )
    regridded_meridional = 0.5 * (
        v_paired[0] + jnp.concatenate([v_cross[:, :, 1:], v_returned[0]], axis=2)
    )
    edge_v = 0.5 * jnp.sum(
        0.5
        * (donor_depths[:, :, -1:] + v_returned[1])
        * meridional_edge_velocity[:, :, -1:]
        * meridional_edge_velocity[:, :, -1:]
    )
    meridional_following = 0.5 * jnp.sum(
        0.5
        * (regridded_depths + jnp.concatenate([regridded_depths[:, :, 1:], v_returned[2]], axis=2))
        * regridded_meridional
        * regridded_meridional
    )
    tracer_new = multiply_by_regrid_operator(
        vertical_regrid_operator, species_means.astype(jnp.float32)
    )
    regridded_warmth = multiply_by_regrid_operator(vertical_regrid_operator, scaled_warmth)
    mass_after = jnp.sum(tracer_new * regridded_depths, axis=(1, 2, 3))
    aggregate_regridded = jnp.sum(regridded_depths)
    kinetic_thermal_following = (
        thermal_rescale_factor * jnp.sum(regridded_depths * regridded_warmth)
        + zonal_following
        + meridional_following
    )
    mass_total_before, mass_total_after, scalars = (
        over_axes(mass_before, GX_GY),
        over_axes(mass_after, GX_GY),
        over_axes(
            jnp.stack(
                [
                    local_prior_totals + edge_u + edge_v,
                    kinetic_thermal_following,
                    aggregate_regridded,
                ]
            ),
            GX_GY,
        ),
    )
    enthalpy_global_preceding = scalars[0]
    enthalpy_global_following = scalars[1]
    thick_total = scalars[2]
    tracers_out = (
        tracer_new + ((mass_total_before - mass_total_after) / thick_total)[:, None, None, None]
    )
    adjusted_warmth = regridded_warmth + (enthalpy_global_preceding - enthalpy_global_following) / (
        thermal_rescale_factor * thick_total
    )
    return (tracers_out, regridded_zonal, regridded_meridional, adjusted_warmth)


def solution(mesh):
    split = Mesh(mesh.devices.reshape(4, 2, 8, 2, 2), ("gx_0", "gx_1", "gy_0", "gy_1", "gy_2"))
    in_specs = (
        P(None, GY, None, GX),
        P(GY, None, GX),
        P(GY, None, GX),
        P(GY, None, GX),
        P(GY, None, GX),
        P(GY, None, GX),
        P(GY, None, GX),
        P(GY, None, GX),
    )
    out_specs = (P(None, GY, None, GX), P(GY, None, GX), P(GY, None, GX), P(GY, None, GX))
    return jax.shard_map(local, mesh=split, in_specs=in_specs, out_specs=out_specs, check_vma=False)
```

profile of v0, /device:TPU:1, one launch (start us, length us, event | category | flops | bytes accessed | tf_op | source)
XLA Modules:
  0.0 101.0 jit_solution(2955615427944298031)
XLA Ops:
  0.6 1.7 %slice.551 = f32[2,120,1]{2,1,0:T(8,128)} slice(f32[2,120,128]{2,1,0:T(8,128)} %param.10), slice={[0:2], [0:120], [127:128]} | slice | bytes 1920 | tf_op jit(solution)/shard_map/slice | solution.py:175
  2.3 3.6 %collective-permute-start.2 = (f32[2,120,1]{2,1,0:T(8,128)}, f32[2,120,1]{2,1,0:T(8,128)S(1)}, u32[]{:S(2)}, u32[]{:S(2)}) collective-permute-start(f32[2,120,1]{2,1,0:T(8,128)} %slice.551), channel_id=1, source_target_pairs={{0,32},{32,64},{64,96},{96,128},{128,160},{160,192},{192,224},{224... | collective-permute-start | bytes 2888 | tf_op jit(solution)/shard_map/ppermute | solution.py:17
  6.5 1.2 %collective-permute-start = (f32[1,120,128]{2,1,0:T(8,128)}, f32[1,120,128]{2,1,0:T(8,128)}, u32[]{:S(2)}, u32[]{:S(2)}) collective-permute-start(f32[1,120,128]{2,1,0:T(8,128)} %get-tuple-element.129), channel_id=1, source_target_pairs={{0,1},{1,2},{2,3},{3,4},{4,5},{5,6},{6,7},{7,8},{8,9},{9,10},{10,1... | collective-permute-start | bytes 184328 | tf_op jit(solution)/shard_map/ppermute | solution.py:17
  7.8 1.0 copy-done.2
  10.9 0.8 copy-done.1
  11.7 0.7 fusion.46
  14.3 0.7 fusion.61
  15.0 0.8 fusion.98
  15.7 0.8 fusion.99
  17.2 0.7 pad_maximum_fusion.20
  17.9 7.7 %multiply_reduce_fusion = (f32[8]{0:T(128)S(1)}, f32[8,2,120,128]{3,2,1,0:T(8,128)S(1)}) fusion(f32[2,120,128]{2,1,0:T(8,128)S(1)} %get-tuple-element.137, f32[2,120,128]{2,1,0:T(8,128)S(1)} %get-tuple-element.153, f32[2,120,128]{2,1,0:T(8,128)S(1)} %get-tuple-element.152, pred[2,120,128]{2,1,0:T(8,128)(4,1)S(1)} %get-tuple-element.139, ...), kind=kLoop, calls=%fused_computation.18 | loop fusion | flops 24084472 | bytes 17244192 | tf_op jit(solution)/shard_map/reduce_sum | solution.py:210
  25.6 0.8 slice.715
  29.7 1.0 add_divide_fusion.1
  30.8 0.8 slice.718
  31.6 3.8 %collective-permute-start.3 = (f32[3,2,120,1]{2,1,3,0:T(2,128)S(1)}, f32[3,2,120,1]{2,1,3,0:T(2,128)S(1)}, u32[]{:S(2)}, u32[]{:S(2)}) collective-permute-start(f32[3,2,120,1]{2,1,3,0:T(2,128)S(1)} %pad_maximum_fusion.23), channel_id=1, source_target_pairs={{0,224},{32,0},{64,32},{96,64},{128,96},{160,128},{192,160},{224,1... | collective-permute-start | bytes 8648 | tf_op jit(solution)/shard_map/ppermute | solution.py:17
  35.4 0.8 maximum_bitcast_fusion
  36.8 1.0 add_divide_fusion.2
  38.7 0.7 pad_maximum_fusion.17
  39.6 0.8 copy.187
  40.4 0.8 copy.188
  41.4 0.7 fusion.47
  42.7 2.0 %collective-permute-done.1 = f32[3,1,120,128]{3,2,1,0:T(8,128)} collective-permute-done((f32[3,1,120,128]{3,2,1,0:T(8,128)}, f32[3,1,120,128]{3,2,1,0:T(8,128)}, u32[]{:S(2)}, u32[]{:S(2)}) %collective-permute-start.1) | collective-permute-done | bytes 184352 | tf_op jit(solution)/shard_map/ppermute | solution.py:17
  44.6 0.9 slice_bitcast_fusion.3
  45.6 3.6 %fusion.49 = (f32[]{:T(128)}, f32[]{:T(128)}, f32[]{:T(128)}, f32[]{:T(128)}, f32[2,120,128]{2,1,0:T(8,128)}, /*index=5*/f32[2,120,128]{2,1,0:T(8,128)}, f32[2,120,128]{2,1,0:T(8,128)}) fusion(f32[2,120,128]{2,1,0:T(8,128)S(1)} %get-tuple-element.137, f32[2,120,1]{2,1,0:T(8,128)} %copy.187, f32[2,120,127]{2,1,0:T(8,128)} %slice.715, ...), kind=kLoop, calls=%fused_computation.136 | loop fusion | flops 3839996 | bytes 3906576 | tf_op jit(solution)/shard_map/reduce_sum | solution.py:200
  51.1 1.5 %fusion.63 = (f32[]{:T(128)}, f32[]{:T(128)}) fusion(f32[3,1,120,128]{3,2,1,0:T(8,128)} %collective-permute-done.1, f32[2,120,128]{2,1,0:T(8,128)S(1)} %copy-done, f32[2,120,128]{2,1,0:T(8,128)S(1)} %copy-done.4), kind=kLoop, calls=%fused_computation.176 | loop fusion | flops 153598 | bytes 307208 | tf_op jit(solution)/shard_map/reduce_sum | solution.py:162
  53.9 0.7 pad_maximum_fusion.24
  54.6 7.5 %all-reduce.66 = (f32[8]{0:T(128)S(1)}, f32[8]{0:T(128)S(1)}, f32[3]{0:T(128)S(1)}) all-reduce(f32[8]{0:T(128)S(1)} %get-tuple-element.79, f32[8]{0:T(128)S(1)} %get-tuple-element.48, f32[3]{0:T(128)S(1)} %pad_maximum_fusion.24), channel_id=1, replica_groups=mesh['gx_0'=4,'gx_1'=2,'gy_0'=8,'gy_1'=2,'gy_2'=2] {'gx_0'}, use_global_device_ids=true, to_apply=%region_1.2 | all-reduce | flops 19 | bytes 152 | tf_op jit(solution)/shard_map/psum | solution.py:22
  62.1 5.3 %all-reduce.69 = (f32[8]{0:T(128)S(1)}, f32[8]{0:T(128)S(1)}, f32[3]{0:T(128)S(1)}) all-reduce(f32[8]{0:T(128)S(1)} %get-tuple-element.21, f32[8]{0:T(128)S(1)} %get-tuple-element.22, f32[3]{0:T(128)S(1)} %get-tuple-element.23), channel_id=1, replica_groups=mesh['gx_0'=4,'gx_1'=2,'gy_0'=8,'gy_1'=2,'gy_2'=2] {'gx_1'}, use_global_device_ids=true, to_apply=%region_2.3 | all-reduce | flops 19 | bytes 152 | tf_op jit(solution)/shard_map/psum | solution.py:22
  67.3 16.3 %all-reduce.65 = (f32[8]{0:T(128)S(1)}, f32[8]{0:T(128)S(1)}, f32[3]{0:T(128)S(1)}) all-reduce(f32[8]{0:T(128)S(1)} %get-tuple-element.30, f32[8]{0:T(128)S(1)} %get-tuple-element.31, f32[3]{0:T(128)S(1)} %get-tuple-element.32), channel_id=1, replica_groups=mesh['gx_0'=4,'gx_1'=2,'gy_0'=8,'gy_1'=2,'gy_2'=2] {'gy_0'}, use_global_device_ids=true, to_apply=%region_3.4 | all-reduce | flops 19 | bytes 152 | tf_op jit(solution)/shard_map/psum | solution.py:22
  83.6 3.8 %all-reduce.68 = (f32[8]{0:T(128)S(1)}, f32[8]{0:T(128)S(1)}, f32[3]{0:T(128)S(1)}) all-reduce(f32[8]{0:T(128)S(1)} %get-tuple-element.18, f32[8]{0:T(128)S(1)} %get-tuple-element.19, f32[3]{0:T(128)S(1)} %get-tuple-element.20), channel_id=1, replica_groups=mesh['gx_0'=4,'gx_1'=2,'gy_0'=8,'gy_1'=2,'gy_2'=2] {'gy_1'}, use_global_device_ids=true, to_apply=%region_4.5 | all-reduce | flops 19 | bytes 152 | tf_op jit(solution)/shard_map/psum | solution.py:22
  87.4 8.6 %all-reduce.67 = (f32[8]{0:T(128)S(1)}, f32[8]{0:T(128)S(1)}, f32[3]{0:T(128)S(1)}) all-reduce(f32[8]{0:T(128)S(1)} %get-tuple-element.27, f32[8]{0:T(128)S(1)} %get-tuple-element.28, f32[3]{0:T(128)S(1)} %get-tuple-element.29), channel_id=1, replica_groups=mesh['gx_0'=4,'gx_1'=2,'gy_0'=8,'gy_1'=2,'gy_2'=2] {'gy_2'}, use_global_device_ids=true, to_apply=%region_5.6 | all-reduce | flops 19 | bytes 152 | tf_op jit(solution)/shard_map/psum | solution.py:22
  97.9 1.1 %broadcast_add_fusion = f32[8,2,120,128]{3,2,1,0:T(8,128)} fusion(f32[8,2,120,128]{3,2,1,0:T(8,128)S(1)} %get-tuple-element.49, f32[8]{0:T(128)S(1)} %subtract_divide_fusion), kind=kLoop, calls=%fused_computation.57 | loop fusion | flops 245760 | bytes 1966112 | tf_op jit(solution)/shard_map/add | solution.py:235
  (98 shorter events, 11.0 us)
Async XLA Ops:
  0.6 5.3 %copy-start.4 = (f32[2,120,128]{2,1,0:T(8,128)S(1)}, f32[2,120,128]{2,1,0:T(8,128)}, u32[]{:S(2)}) copy-start(f32[2,120,128]{2,1,0:T(8,128)} %param.9) | copy-start | bytes 368644
  2.3 5.4 %copy-start = (f32[2,120,128]{2,1,0:T(8,128)S(1)}, f32[2,120,128]{2,1,0:T(8,128)}, u32[]{:S(2)}) copy-start(f32[2,120,128]{2,1,0:T(8,128)} %param.12) | copy-start | bytes 368644
  2.3 26.7 %collective-permute-start.2 = (f32[2,120,1]{2,1,0:T(8,128)}, f32[2,120,1]{2,1,0:T(8,128)S(1)}, u32[]{:S(2)}, u32[]{:S(2)}) collective-permute-start(f32[2,120,1]{2,1,0:T(8,128)} %slice.551), channel_id=1, source_target_pairs={{0,32},{32,64},{64,96},{96,128},{128,160},{160,192},{192,224},{224... | collective-permute-start | bytes 2888 | tf_op jit(solution)/shard_map/ppermute | solution.py:17
  6.5 28.9 %collective-permute-start = (f32[1,120,128]{2,1,0:T(8,128)}, f32[1,120,128]{2,1,0:T(8,128)}, u32[]{:S(2)}, u32[]{:S(2)}) collective-permute-start(f32[1,120,128]{2,1,0:T(8,128)} %get-tuple-element.129), channel_id=1, source_target_pairs={{0,1},{1,2},{2,3},{3,4},{4,5},{5,6},{6,7},{7,8},{8,9},{9,10},{10,1... | collective-permute-start | bytes 184328 | tf_op jit(solution)/shard_map/ppermute | solution.py:17
  7.7 1.0 %copy-start.2 = (bf16[8,2,120,128]{3,2,1,0:T(8,128)(2,1)S(1)}, bf16[8,2,120,128]{3,2,1,0:T(8,128)(2,1)}, u32[]{:S(2)}) copy-start(bf16[8,2,120,128]{3,2,1,0:T(8,128)(2,1)} %param.8) | copy-start | bytes 1474564
  10.8 0.9 copy-start.1
  11.7 0.8 copy-start.12
  11.7 0.9 copy-start.13
  11.7 1.0 copy-start.15
  13.2 1.0 copy-start.3
  31.6 8.0 %collective-permute-start.3 = (f32[3,2,120,1]{2,1,3,0:T(2,128)S(1)}, f32[3,2,120,1]{2,1,3,0:T(2,128)S(1)}, u32[]{:S(2)}, u32[]{:S(2)}) collective-permute-start(f32[3,2,120,1]{2,1,3,0:T(2,128)S(1)} %pad_maximum_fusion.23), channel_id=1, source_target_pairs={{0,224},{32,0},{64,32},{96,64},{128,96},{160,128},{192,160},{224,1... | collective-permute-start | bytes 8648 | tf_op jit(solution)/shard_map/ppermute | solution.py:17
  37.8 0.8 copy-start.11
  39.4 5.3 %collective-permute-start.1 = (f32[3,1,120,128]{3,2,1,0:T(8,128)}, f32[3,1,120,128]{3,2,1,0:T(8,128)}, u32[]{:S(2)}, u32[]{:S(2)}) collective-permute-start(f32[3,1,120,128]{3,2,1,0:T(8,128)} %pad_maximum_fusion.17), channel_id=1, source_target_pairs={{0,31},{1,0},{2,1},{3,2},{4,3},{5,4},{6,5},{7,6},{8,7},{9,8},{10,9... | collective-permute-start | bytes 552968 | tf_op jit(solution)/shard_map/ppermute | solution.py:17
  40.4 5.1 %copy-start.7 = (f32[2,118,128]{2,1,0:T(8,128)S(1)}, f32[2,118,128]{2,1,0:T(8,128)}, u32[]{:S(2)}) copy-start(f32[2,118,128]{2,1,0:T(8,128)} %get-tuple-element.168) | copy-start | bytes 362500
  40.4 5.1 %copy-start.8 = (f32[2,118,128]{2,1,0:T(8,128)S(1)}, f32[2,118,128]{2,1,0:T(8,128)}, u32[]{:S(2)}) copy-start(f32[2,118,128]{2,1,0:T(8,128)} %get-tuple-element.169) | copy-start | bytes 362500
  40.4 5.1 %copy-start.14 = (f32[1,120,128]{2,1,0:T(8,128)S(1)}, f32[1,120,128]{2,1,0:T(8,128)}, u32[]{:S(2)}) copy-start(f32[1,120,128]{2,1,0:T(8,128)} %get-tuple-element.127) | copy-start | bytes 184324
  41.2 4.3 %copy-start.9 = (f32[2,119,128]{2,1,0:T(8,128)S(1)}, f32[2,119,128]{2,1,0:T(8,128)}, u32[]{:S(2)}) copy-start(f32[2,119,128]{2,1,0:T(8,128)} %get-tuple-element.121) | copy-start | bytes 365572
  42.6 2.9 %copy-start.5 = (f32[2,118,128]{2,1,0:T(8,128)S(1)}, f32[2,118,128]{2,1,0:T(8,128)}, u32[]{:S(2)}) copy-start(f32[2,118,128]{2,1,0:T(8,128)} %get-tuple-element.119) | copy-start | bytes 362500
  42.7 2.9 %copy-start.6 = (f32[2,118,128]{2,1,0:T(8,128)S(1)}, f32[2,118,128]{2,1,0:T(8,128)}, u32[]{:S(2)}) copy-start(f32[2,118,128]{2,1,0:T(8,128)} %get-tuple-element.120) | copy-start | bytes 362500
  97.8 2.5 %copy-start.10 = (f32[2,120,128]{2,1,0:T(8,128)S(1)}, f32[2,120,128]{2,1,0:T(8,128)}, u32[]{:S(2)}) copy-start(f32[2,120,128]{2,1,0:T(8,128)} %get-tuple-element.33) | copy-start | bytes 368644
where the time goes:
time: 102 us; the launch traced here: 101 us
  blocking collectives  41.4 us (41%)
  other arithmetic  25.3 us (25%)
  local copies, waits for them, and re-layouts  15.3 us (15%)
  starting transfers between devices  8.84 us (9%)
  between operations  8.16 us (8%)
  waiting for transfers between devices  1.97 us (2%)
    psum x5, blocking collectives, over_axes(): x = lax.psum(x, axis)  41.4 us
    ppermute x4, starting transfers between devices, passed_along(): return lax.ppermute(value, axis, pairs)  8.84 us
    reduce_sum x1, other arithmetic, local(): mass_after = jnp.sum(tracer_new * regridded_depths, axis=(1, 2, 3))  7.73 us
    reduce_sum x1, other arithmetic, local(): jnp.sum(0.5 * (regridded_depths + jnp.concatenate([regridded_depths[:, :,...  3.63 us
    slice x14, local copies, waits for them, and re-layouts, shifted_layers(): return jnp.concatenate([filler, values[..., :layers + amount, :]], axis=-2)  2.61 us
    unnamed x33, local copies, waits for them, and re-layouts  2.61 us
  transfers between devices with their start and end apart: 4, of which 1 were waited for; matrix products, arithmetic and copies ran while one was open for 26% of the time, Pallas kernels for 0%

commit v1 on v0

--- a/solution.py
+++ b/solution.py
@@ -19,7 +19,7 @@
 
 def over_axes(x, axes):
     for axis in axes:
-        x = lax.psum(x, axis)
+        x = jnp.sum(lax.all_gather(x, axis), axis=0)
     return x
 
 

time: 102 us -> 136 us (1.33)
  local copies, waits for them, and re-layouts: 15.3 us -> 35.6 us
  between operations: 8.16 us -> 15.2 us
  other arithmetic: 25.3 us -> 31.9 us
    unnamed x0 -> x5, blocking collectives: none -> 41.5 us
    psum x5 -> x0, blocking collectives: 41.4 us -> none  [over_axes(): x = lax.psum(x, axis)]
    unnamed x33 -> x157, local copies, waits for them, and re-layouts: 2.61 us -> 16.1 us
    slice x14, local copies, waits for them, and re-layouts: 2.61 us -> 5.98 us  [shifted_layers(): return jnp.concatenate([filler, values[..., :layers + amount, :]], axis=-2)]
    concatenate x12, other arithmetic: 1.74 us -> 4.34 us  [ppm_parts(): jnp.concatenate([top_edge, second_edge, inner_edge, lower_edge, bottom_ed...]
    slice x9, local copies, waits for them, and re-layouts: 1.56 us -> 3.48 us  [shifted_layers(): return jnp.concatenate([values[..., amount:, :], filler], axis=-2)]
  transfers between devices with their start and end apart: 4 -> 4, of which waited for: 1 -> 1; matrix products, arithmetic and copies ran while one was open for 26% -> 34% of each run, Pallas kernels for 0% -> 0%
where the time goes in v1:
time: 136 us; the launch traced here: 135 us
  blocking collectives  41.5 us (31%)
  local copies, waits for them, and re-layouts  35.6 us (26%)
  other arithmetic  31.9 us (23%)
  between operations  15.2 us (11%)
  starting transfers between devices  8.92 us (7%)
  waiting for transfers between devices  1.47 us (1%)
    unnamed x5, blocking collectives  41.5 us
    unnamed x157, local copies, waits for them, and re-layouts  16.1 us
    reduce_sum x1, other arithmetic, local(): mass_after = jnp.sum(tracer_new * regridded_depths, axis=(1, 2, 3))  9.08 us
    ppermute x4, starting transfers between devices, passed_along(): return lax.ppermute(value, axis, pairs)  8.92 us
    slice x14, local copies, waits for them, and re-layouts, shifted_layers(): return jnp.concatenate([filler, values[..., :layers + amount, :]], axis=-2)  5.98 us
    concatenate x12, other arithmetic, ppm_parts(): jnp.concatenate([top_edge, second_edge, inner_edge, lower_edge, bottom_ed...  4.34 us
    reduce_sum x1, other arithmetic, local(): jnp.sum(0.5 * (regridded_depths + jnp.concatenate([regridded_depths[:, :,...  3.64 us
    slice x9, local copies, waits for them, and re-layouts, shifted_layers(): return jnp.concatenate([values[..., amount:, :], filler], axis=-2)  3.48 us
  transfers between devices with their start and end apart: 4, of which 1 were waited for; matrix products, arithmetic and copies ran while one was open for 34% of the time, Pallas kernels for 0%

profile of v1, /device:TPU:1, one launch (start us, length us, event | category | flops | bytes accessed | tf_op | source)
XLA Modules:
  0.0 134.6 jit_solution(13448924127715643606)
XLA Ops:
  0.6 1.7 %slice.551 = f32[2,120,1]{2,1,0:T(8,128)} slice(f32[2,120,128]{2,1,0:T(8,128)} %param.10), slice={[0:2], [0:120], [127:128]} | slice | bytes 1920 | tf_op jit(solution)/shard_map/slice | solution.py:175
  2.3 3.6 %collective-permute-start.2 = (f32[2,120,1]{2,1,0:T(8,128)}, f32[2,120,1]{2,1,0:T(8,128)}, u32[]{:S(2)}, u32[]{:S(2)}) collective-permute-start(f32[2,120,1]{2,1,0:T(8,128)} %slice.551), channel_id=1, source_target_pairs={{0,32},{32,64},{64,96},{96,128},{128,160},{160,192},{192,224},{224... | collective-permute-start | bytes 2888 | tf_op jit(solution)/shard_map/ppermute | solution.py:17
  6.5 1.2 collective-permute-start
  7.8 1.0 copy-done.2
  9.5 1.1 fusion.7
  10.5 1.0 slice.631
  11.5 2.0 %fusion.86 = (f32[8,2,118,128]{3,2,1,0:T(8,128)}, f32[8,2,118,128]{3,2,1,0:T(8,128)}, f32[8,2,118,128]{3,2,1,0:T(8,128)}, f32[8,2,118,128]{3,2,1,0:T(8,128)}) fusion(f32[8,2,120,128]{3,2,1,0:T(8,128)S(1)} %get-tuple-element.65, f32[8,2,120,128]{3,2,1,0:T(8,128)S(1)} %get-tuple-element.66), kind=kLoop, calls=%fused_computation.223 | loop fusion | bytes 7733248 | tf_op jit(solution)/shard_map/slice | solution.py:55
  13.6 2.0 %fusion.87 = (f32[8,2,119,128]{3,2,1,0:T(8,128)}, f32[8,2,119,128]{3,2,1,0:T(8,128)}, f32[8,2,119,128]{3,2,1,0:T(8,128)}, f32[8,2,119,128]{3,2,1,0:T(8,128)}) fusion(f32[8,2,120,128]{3,2,1,0:T(8,128)S(1)} %get-tuple-element.65, f32[8,2,120,128]{3,2,1,0:T(8,128)S(1)} %get-tuple-element.66), kind=kLoop, calls=%fused_computation.224 | loop fusion | bytes 7798784 | tf_op jit(solution)/shard_map/slice | solution.py:55
  15.6 1.1 slice.626
  16.7 1.1 fusion
  17.7 1.0 pad_maximum_fusion.2
  19.7 1.3 fusion.46
  21.0 1.2 fusion.51
  31.2 1.3 dynamic-slice
  35.9 1.3 dynamic-slice.2
  38.5 1.2 dynamic-slice.3
  40.9 1.3 dynamic-slice.4
  42.2 9.1 %multiply_reduce_fusion = (f32[8]{0:T(128)}, f32[8,2,120,128]{3,2,1,0:T(8,128)}) fusion(f32[2,120,128]{2,1,0:T(8,128)S(1)} %get-tuple-element.137, f32[2,120,128]{2,1,0:T(8,128)} %get-tuple-element.153, f32[2,120,128]{2,1,0:T(8,128)} %get-tuple-element.152, pred[2,120,128]{2,1,0:T(8,128)(4,1)S(1)} %get-tuple-element.139, ...), kind=kLoop, calls=%fused_computation.18 | loop fusion | flops 24084472 | bytes 17244192 | tf_op jit(solution)/shard_map/reduce_sum | solution.py:210
  55.6 1.0 maximum_bitcast_fusion.1
  58.4 1.0 add_divide_fusion.1
  60.9 3.8 %collective-permute-start.3 = (f32[3,2,120,1]{2,1,3,0:T(2,128)S(1)}, f32[3,2,120,1]{2,1,3,0:T(2,128)S(1)}, u32[]{:S(2)}, u32[]{:S(2)}) collective-permute-start(f32[3,2,120,1]{2,1,3,0:T(2,128)S(1)} %pad_maximum_fusion.23), channel_id=1, source_target_pairs={{0,224},{32,0},{64,32},{96,64},{128,96},{160,128},{192,160},{224,1... | collective-permute-start | bytes 8648 | tf_op jit(solution)/shard_map/ppermute | solution.py:17
  64.7 0.8 maximum_bitcast_fusion
  66.1 1.0 add_divide_fusion.2
  71.6 1.5 %collective-permute-done.1 = f32[3,1,120,128]{3,2,1,0:T(8,128)S(1)} collective-permute-done((f32[3,1,120,128]{3,2,1,0:T(8,128)S(1)}, f32[3,1,120,128]{3,2,1,0:T(8,128)S(1)}, u32[]{:S(2)}, u32[]{:S(2)}) %collective-permute-start.1) | collective-permute-done | bytes 184352 | tf_op jit(solution)/shard_map/ppermute | solution.py:17
  74.4 3.6 %fusion.49 = (f32[]{:T(128)}, f32[]{:T(128)}, f32[]{:T(128)}, f32[]{:T(128)}, f32[2,120,128]{2,1,0:T(8,128)}, /*index=5*/f32[2,120,128]{2,1,0:T(8,128)}, f32[2,120,128]{2,1,0:T(8,128)}) fusion(f32[2,120,128]{2,1,0:T(8,128)S(1)} %get-tuple-element.137, f32[2,120,1]{2,1,0:T(8,128)} %copy.187, f32[2,120,127]{2,1,0:T(8,128)S(1)} %copy-done.31, ...), kind=kLoop, calls=%fused_computation.136 | loop fusion | flops 3839996 | bytes 3906576 | tf_op jit(solution)/shard_map/reduce_sum | solution.py:200
  80.1 1.5 %fusion.63 = (f32[]{:T(128)}, f32[]{:T(128)}) fusion(f32[3,1,120,128]{3,2,1,0:T(8,128)} %copy-done.44, f32[2,120,128]{2,1,0:T(8,128)S(1)} %copy-done, f32[2,120,128]{2,1,0:T(8,128)S(1)} %copy-done.5), kind=kLoop, calls=%fused_computation.176 | loop fusion | flops 153598 | bytes 307208 | tf_op jit(solution)/shard_map/reduce_sum | solution.py:162
  83.8 7.5 %all-reduce.81 = (f32[32]{0:T(128)S(1)}, f32[32]{0:T(128)S(1)}, f32[12]{0:T(128)S(1)}) all-reduce(f32[32]{0:T(128)S(1)} %dynamic-update-slice, f32[32]{0:T(128)S(1)} %dynamic-update-slice.5, f32[12]{0:T(128)S(1)} %maximum_dynamic-update-slice_fusion), channel_id=2, replica_groups=mesh['gx_0'=4,'gx_1'=2,'gy_0'=8,'gy_1'=2,'gy_2'=2] {'gx_0'}, use_global_device_ids=true, to_apply=%add.65 | all-reduce | flops 76 | bytes 608
  92.3 5.3 %all-reduce.84 = (f32[16]{0:T(128)S(1)}, f32[16]{0:T(128)S(1)}, f32[6]{0:T(128)S(1)}) all-reduce(f32[16]{0:T(128)S(1)} %dynamic-update-slice.1, f32[16]{0:T(128)S(1)} %dynamic-update-slice.6, f32[6]{0:T(128)S(1)} %dynamic-update-slice.11), channel_id=3, replica_groups=mesh['gx_0'=4,'gx_1'=2,'gy_0'=8,'gy_1'=2,'gy_2'=2] {'gx_1'}, use_global_device_ids=true, to_apply=%add.66 | all-reduce | flops 38 | bytes 304
  98.5 16.5 %all-reduce.80 = (f32[64]{0:T(128)S(1)}, f32[64]{0:T(128)S(1)}, f32[24]{0:T(128)S(1)}) all-reduce(f32[64]{0:T(128)S(1)} %dynamic-update-slice.2, f32[64]{0:T(128)S(1)} %dynamic-update-slice.7, f32[24]{0:T(128)S(1)} %dynamic-update-slice.12), channel_id=4, replica_groups=mesh['gx_0'=4,'gx_1'=2,'gy_0'=8,'gy_1'=2,'gy_2'=2] {'gy_0'}, use_global_device_ids=true, to_apply=%add.67 | all-reduce | flops 152 | bytes 1216
  116.0 3.9 %all-reduce.83 = (f32[16]{0:T(128)S(1)}, f32[16]{0:T(128)S(1)}, f32[6]{0:T(128)S(1)}) all-reduce(f32[16]{0:T(128)S(1)} %dynamic-update-slice.3, f32[16]{0:T(128)S(1)} %dynamic-update-slice.8, f32[6]{0:T(128)S(1)} %dynamic-update-slice.13), channel_id=5, replica_groups=mesh['gx_0'=4,'gx_1'=2,'gy_0'=8,'gy_1'=2,'gy_2'=2] {'gy_1'}, use_global_device_ids=true, to_apply=%add.68 | all-reduce | flops 38 | bytes 304
  120.9 8.5 %all-reduce.82 = (f32[16]{0:T(128)S(1)}, f32[16]{0:T(128)S(1)}, f32[6]{0:T(128)S(1)}) all-reduce(f32[16]{0:T(128)S(1)} %dynamic-update-slice.4, f32[16]{0:T(128)S(1)} %dynamic-update-slice.9, f32[6]{0:T(128)S(1)} %dynamic-update-slice.14), channel_id=6, replica_groups=mesh['gx_0'=4,'gx_1'=2,'gy_0'=8,'gy_1'=2,'gy_2'=2] {'gy_2'}, use_global_device_ids=true, to_apply=%add.69 | all-reduce | flops 38 | bytes 304
  131.6 1.1 broadcast_add_fusion
  (252 shorter events, 29.2 us)
Async XLA Ops:
  0.6 5.3 %copy-start.5 = (f32[2,120,128]{2,1,0:T(8,128)S(1)}, f32[2,120,128]{2,1,0:T(8,128)}, u32[]{:S(2)}) copy-start(f32[2,120,128]{2,1,0:T(8,128)} %param.9) | copy-start | bytes 368644
  2.3 5.4 %copy-start = (f32[2,120,128]{2,1,0:T(8,128)S(1)}, f32[2,120,128]{2,1,0:T(8,128)}, u32[]{:S(2)}) copy-start(f32[2,120,128]{2,1,0:T(8,128)} %param.12) | copy-start | bytes 368644
  2.3 53.3 %collective-permute-start.2 = (f32[2,120,1]{2,1,0:T(8,128)}, f32[2,120,1]{2,1,0:T(8,128)}, u32[]{:S(2)}, u32[]{:S(2)}) collective-permute-start(f32[2,120,1]{2,1,0:T(8,128)} %slice.551), channel_id=1, source_target_pairs={{0,32},{32,64},{64,96},{96,128},{128,160},{160,192},{192,224},{224... | collective-permute-start | bytes 2888 | tf_op jit(solution)/shard_map/ppermute | solution.py:17
  6.5 58.2 %collective-permute-start = (f32[1,120,128]{2,1,0:T(8,128)}, f32[1,120,128]{2,1,0:T(8,128)}, u32[]{:S(2)}, u32[]{:S(2)}) collective-permute-start(f32[1,120,128]{2,1,0:T(8,128)} %get-tuple-element.129), channel_id=1, source_target_pairs={{0,1},{1,2},{2,3},{3,4},{4,5},{5,6},{6,7},{7,8},{8,9},{9,10},{10,1... | collective-permute-start | bytes 184328 | tf_op jit(solution)/shard_map/ppermute | solution.py:17
  8.9 9.9 %copy-start.45 = (f32[8,2,1,128]{3,2,1,0:T(1,128)}, f32[8,2,1,128]{3,2,1,0:T(1,128)S(1)}, u32[]{:S(2)}) copy-start(f32[8,2,1,128]{3,2,1,0:T(1,128)S(1)} %get-tuple-element.78) | copy-start | bytes 24580
  24.9 4.9 %copy-start.49 = (f32[2,1,128]{2,1,0:T(1,128)}, f32[2,1,128]{2,1,0:T(1,128)S(1)}, u32[]{:S(2)}) copy-start(f32[2,1,128]{2,1,0:T(1,128)S(1)} %get-tuple-element.114) | copy-start | bytes 3076
  25.0 5.6 %copy-start.51 = (f32[2,1,128]{2,1,0:T(1,128)}, f32[2,1,128]{2,1,0:T(1,128)S(1)}, u32[]{:S(2)}) copy-start(f32[2,1,128]{2,1,0:T(1,128)S(1)} %get-tuple-element.112) | copy-start | bytes 3076
  25.0 5.6 %copy-start.53 = (f32[2,1,128]{2,1,0:T(1,128)}, f32[2,1,128]{2,1,0:T(1,128)S(1)}, u32[]{:S(2)}) copy-start(f32[2,1,128]{2,1,0:T(1,128)S(1)} %get-tuple-element.115) | copy-start | bytes 3076
  34.5 7.7 %copy-start.46 = (f32[8,2,1,128]{3,2,1,0:T(1,128)S(1)}, f32[8,2,1,128]{3,2,1,0:T(1,128)}, u32[]{:S(2)}) copy-start(f32[8,2,1,128]{3,2,1,0:T(1,128)} %copy-done.45) | copy-start | bytes 24580
  37.8 4.3 %copy-start.11 = (pred[2,120,128]{2,1,0:T(8,128)(4,1)S(1)}, pred[2,120,128]{2,1,0:T(8,128)(4,1)}, u32[]{:S(2)}) copy-start(pred[2,120,128]{2,1,0:T(8,128)(4,1)} %get-tuple-element.142) | copy-start | bytes 92164
  37.8 4.3 %copy-start.14 = (pred[2,120,128]{2,1,0:T(8,128)(4,1)S(1)}, pred[2,120,128]{2,1,0:T(8,128)(4,1)}, u32[]{:S(2)}) copy-start(pred[2,120,128]{2,1,0:T(8,128)(4,1)} %get-tuple-element.143) | copy-start | bytes 92164
  51.3 4.3 %copy-start.37 = (f32[2,120,127]{2,1,0:T(8,128)S(1)}, f32[2,120,127]{2,1,0:T(8,128)}, u32[]{:S(2)}) copy-start(f32[2,120,127]{2,1,0:T(8,128)} %get-tuple-element.118) | copy-start | bytes 365764
  59.5 5.2 %copy-start.40 = (f32[1,120,128]{2,1,0:T(8,128)S(1)}, f32[1,120,128]{2,1,0:T(8,128)}, u32[]{:S(2)}) copy-start(f32[1,120,128]{2,1,0:T(8,128)} %get-tuple-element.130) | copy-start | bytes 184324
  60.9 7.5 %collective-permute-start.3 = (f32[3,2,120,1]{2,1,3,0:T(2,128)S(1)}, f32[3,2,120,1]{2,1,3,0:T(2,128)S(1)}, u32[]{:S(2)}, u32[]{:S(2)}) collective-permute-start(f32[3,2,120,1]{2,1,3,0:T(2,128)S(1)} %pad_maximum_fusion.23), channel_id=1, source_target_pairs={{0,224},{32,0},{64,32},{96,64},{128,96},{160,128},{192,160},{224,1... | collective-permute-start | bytes 8648 | tf_op jit(solution)/shard_map/ppermute | solution.py:17
  68.0 5.7 %copy-start.33 = (f32[2,118,128]{2,1,0:T(8,128)S(1)}, f32[2,118,128]{2,1,0:T(8,128)}, u32[]{:S(2)}) copy-start(f32[2,118,128]{2,1,0:T(8,128)} %get-tuple-element.119) | copy-start | bytes 362500
  68.0 5.7 %copy-start.34 = (f32[2,118,128]{2,1,0:T(8,128)S(1)}, f32[2,118,128]{2,1,0:T(8,128)}, u32[]{:S(2)}) copy-start(f32[2,118,128]{2,1,0:T(8,128)} %get-tuple-element.120) | copy-start | bytes 362500
  68.0 5.7 %copy-start.35 = (f32[2,118,128]{2,1,0:T(8,128)S(1)}, f32[2,118,128]{2,1,0:T(8,128)}, u32[]{:S(2)}) copy-start(f32[2,118,128]{2,1,0:T(8,128)} %get-tuple-element.168) | copy-start | bytes 362500
  68.0 5.0 %collective-permute-start.1 = (f32[3,1,120,128]{3,2,1,0:T(8,128)S(1)}, f32[3,1,120,128]{3,2,1,0:T(8,128)S(1)}, u32[]{:S(2)}, u32[]{:S(2)}) collective-permute-start(f32[3,1,120,128]{3,2,1,0:T(8,128)S(1)} %pad_maximum_fusion.17), channel_id=1, source_target_pairs={{0,31},{1,0},{2,1},{3,2},{4,3},{5,4},{6,5},{7,6},{8,7},{9,8},{10,9... | collective-permute-start | bytes 552968 | tf_op jit(solution)/shard_map/ppermute | solution.py:17
  70.0 3.8 %copy-start.31 = (f32[2,120,127]{2,1,0:T(8,128)S(1)}, f32[2,120,127]{2,1,0:T(8,128)}, u32[]{:S(2)}) copy-start(f32[2,120,127]{2,1,0:T(8,128)} %slice.715) | copy-start | bytes 365764
  70.0 3.8 %copy-start.32 = (f32[2,117,128]{2,1,0:T(8,128)S(1)}, f32[2,117,128]{2,1,0:T(8,128)}, u32[]{:S(2)}) copy-start(f32[2,117,128]{2,1,0:T(8,128)} %slice.709) | copy-start | bytes 359428
  70.0 3.8 %copy-start.42 = (bf16[2,120,128]{2,1,0:T(8,128)(2,1)S(1)}, bf16[2,120,128]{2,1,0:T(8,128)(2,1)}, u32[]{:S(2)}) copy-start(bf16[2,120,128]{2,1,0:T(8,128)(2,1)} %param.14) | copy-start | bytes 184324
  70.1 3.7 %copy-start.22 = (pred[2,120,128]{2,1,0:T(8,128)(4,1)S(1)}, pred[2,120,128]{2,1,0:T(8,128)(4,1)}, u32[]{:S(2)}) copy-start(pred[2,120,128]{2,1,0:T(8,128)(4,1)} %get-tuple-element.147) | copy-start | bytes 92164
  70.1 3.7 %copy-start.24 = (pred[2,120,128]{2,1,0:T(8,128)(4,1)S(1)}, pred[2,120,128]{2,1,0:T(8,128)(4,1)}, u32[]{:S(2)}) copy-start(pred[2,120,128]{2,1,0:T(8,128)(4,1)} %get-tuple-element.148) | copy-start | bytes 92164
  70.1 3.7 %copy-start.26 = (pred[2,120,128]{2,1,0:T(8,128)(4,1)S(1)}, pred[2,120,128]{2,1,0:T(8,128)(4,1)}, u32[]{:S(2)}) copy-start(pred[2,120,128]{2,1,0:T(8,128)(4,1)} %get-tuple-element.149) | copy-start | bytes 92164
  70.1 3.7 %copy-start.28 = (pred[2,120,128]{2,1,0:T(8,128)(4,1)S(1)}, pred[2,120,128]{2,1,0:T(8,128)(4,1)}, u32[]{:S(2)}) copy-start(pred[2,120,128]{2,1,0:T(8,128)(4,1)} %get-tuple-element.150) | copy-start | bytes 92164
  70.2 3.7 %copy-start.30 = (pred[2,120,128]{2,1,0:T(8,128)(4,1)S(1)}, pred[2,120,128]{2,1,0:T(8,128)(4,1)}, u32[]{:S(2)}) copy-start(pred[2,120,128]{2,1,0:T(8,128)(4,1)} %get-tuple-element.151) | copy-start | bytes 92164
  70.2 3.7 %copy-start.52 = (f32[2,1,128]{2,1,0:T(1,128)S(1)}, f32[2,1,128]{2,1,0:T(1,128)}, u32[]{:S(2)}) copy-start(f32[2,1,128]{2,1,0:T(1,128)} %copy-done.51) | copy-start | bytes 3076
  70.2 3.7 %copy-start.54 = (f32[2,1,128]{2,1,0:T(1,128)S(1)}, f32[2,1,128]{2,1,0:T(1,128)}, u32[]{:S(2)}) copy-start(f32[2,1,128]{2,1,0:T(1,128)} %copy-done.53) | copy-start | bytes 3076
  70.2 3.7 %copy-start.56 = (f32[2,1,128]{2,1,0:T(1,128)S(1)}, f32[2,1,128]{2,1,0:T(1,128)}, u32[]{:S(2)}) copy-start(f32[2,1,128]{2,1,0:T(1,128)} %copy-done.55) | copy-start | bytes 3076
  71.6 2.3 %copy-start.10 = (f32[2,119,128]{2,1,0:T(8,128)S(1)}, f32[2,119,128]{2,1,0:T(8,128)}, u32[]{:S(2)}) copy-start(f32[2,119,128]{2,1,0:T(8,128)} %pad_maximum_fusion.21) | copy-start | bytes 365572
  74.4 57.1 %copy-start.3 = (f32[8,2,120,128]{3,2,1,0:T(8,128)S(1)}, f32[8,2,120,128]{3,2,1,0:T(8,128)}, u32[]{:S(2)}) copy-start(f32[8,2,120,128]{3,2,1,0:T(8,128)} %get-tuple-element.49) | copy-start | bytes 2949124
  131.5 2.4 %copy-start.36 = (f32[2,120,128]{2,1,0:T(8,128)S(1)}, f32[2,120,128]{2,1,0:T(8,128)}, u32[]{:S(2)}) copy-start(f32[2,120,128]{2,1,0:T(8,128)} %get-tuple-element.33) | copy-start | bytes 368644
  (33 other events, 28.5 us)
